TPU v7x, 32 devices: a whole 2x2x4 slice. The times are simulated.
32 devices in a mesh: cuts: 2 (over x), ma: 8 (over z, y), mb: 2 (over core).
Axes of the slice: x: 2, y: 2, z: 4, core: 2. Of those that a mesh axis runs over, the one named last changes fastest.
Arguments:
- stem_field: bfloat16 [64, 512, 2, 512], P(('cuts', 'ma', 'mb')), parts along dimension 0, may hold values from -6 to 6
- first_branch_tensors: bfloat16 [2, 2, 512, 512], P(None, None, 'ma'), may hold values from -0.1875 to 0.1875
- second_branch_tensors: bfloat16 [2, 2, 512, 512], P(None, None, 'ma'), may hold values from -0.1875 to 0.1875
- relabel: int32 [2, 512], replicated, may hold values from 0 to 511, each once within a row
- sample_block: int32 [8192, 1], P(('cuts', 'ma', 'mb')), parts along dimension 0, may hold values from 0 to 31; in each aligned block of 256 rows (0 to 255, 256 to 511, ...) at most 16 rows name the same one
- sample_state: bfloat16 [8192, 2, 512], P(('cuts', 'ma', 'mb')), parts along dimension 0, may hold values from -0.1875 to 0.1875
Outputs:
- amplitudes: bfloat16 [8192, 2, 512], P(('cuts', 'ma', 'mb')), parts along dimension 0
There are 2 independent parts, one for each index of `cuts`. A program takes and returns all parts, laid end to end along the dimension named above; an argument that names none is the same for every part. Nothing has to cross between parts.
Inputs may be any that keep to these rules, and one draw needn't show every extreme that they name: `relabel`: each row is a permutation of 0 to 511. `sample_block`: within the 256 rows of one device no prefix block is named more than 16 times.
All inputs are finite; a program needn't handle non-finite values.
Results may differ from a plain program's by a relative error of at most 0.0075.
Values may be sent and summed in bfloat16 or wider, within the bound.
No kernel may reach another device: no remote copies, remote signals or barrier semaphores. Data moves between devices by JAX's collectives and lax.ppermute only.
A program may use at most 64 MiB of HBM per device.

v0:
```python
import jax
import jax.numpy as jnp
from jax import lax
from jax.sharding import PartitionSpec as P


def complex_table(matrix):
    real_part = matrix[0]
    imag_part = matrix[1]
    upper_rows = jnp.stack([real_part, imag_part], axis=1)
    lower_rows = jnp.stack([-imag_part, real_part], axis=1)
    return jnp.stack([upper_rows, lower_rows], axis=0)


def regroup(stem_field):
    blocks, row_count, part_count, col_count = stem_field.shape
    first_count = lax.axis_size("ma")
    second_count = lax.axis_size("mb")
    groups = first_count * second_count
    pieces = stem_field.reshape(blocks, groups, row_count // groups, part_count, col_count)
    swapped_modes = lax.all_to_all(pieces, ("ma", "mb"), split_axis=1, concat_axis=1, tiled=True)
    return swapped_modes.reshape(blocks, row_count, part_count, col_count)


def on_device(
    stem_field, first_branch_tensors, second_branch_tensors, relabel, sample_block, sample_state
):
    rounds = first_branch_tensors.shape[0]
    width_first = first_branch_tensors.shape[3]
    every_first, every_second = (
        lax.all_gather(first_branch_tensors, "ma", axis=2, tiled=True),
        lax.all_gather(second_branch_tensors, "ma", axis=2, tiled=True),
    )
    positions = jnp.arange(width_first, dtype=jnp.int32)
    for regroup_round_index in range(rounds):
        stem_field = regroup(stem_field)
        first_matrix = every_first[regroup_round_index]
        second_matrix = every_second[regroup_round_index]
        selector = (relabel[regroup_round_index][:, None] == positions[None, :]).astype(
            jnp.bfloat16
        )
        permuted = jnp.einsum(
            "ij,pio->pjo", selector, first_matrix, preferred_element_type=jnp.float32
        ).astype(jnp.bfloat16)
        stem_field = jnp.einsum(
            "sapb,paqo->soqb",
            stem_field,
            complex_table(permuted),
            preferred_element_type=jnp.float32,
        ).astype(jnp.bfloat16)
        stem_field = jnp.einsum(
            "sapb,pbqo->saqo",
            stem_field,
            complex_table(second_matrix),
            preferred_element_type=jnp.float32,
        ).astype(jnp.bfloat16)
    local_blocks = stem_field.shape[0]
    groups = lax.axis_size("ma") * lax.axis_size("mb")
    block_count = local_blocks * groups
    samples = sample_state.shape[0]
    slot_bound = max(2, 2 * samples // block_count)
    state_width = sample_state.shape[2]
    owner_block = sample_block[:, 0]
    block_hot = (owner_block[:, None] == jnp.arange(block_count, dtype=jnp.int32)[None, :]).astype(
        jnp.bfloat16
    )
    order_index = jnp.arange(samples, dtype=jnp.int32)
    earlier_mask = (order_index[:, None] > order_index[None, :]).astype(jnp.bfloat16)
    earlier = jnp.dot(earlier_mask, block_hot, preferred_element_type=jnp.float32)
    slot_index = jnp.sum(earlier * block_hot.astype(jnp.float32), axis=1)
    slot_hot = (slot_index[:, None] == jnp.arange(slot_bound, dtype=jnp.float32)[None, :]).astype(
        jnp.bfloat16
    )
    dispatch = (block_hot[:, :, None] * slot_hot[:, None, :]).reshape(
        samples, block_count * slot_bound
    )
    outgoing = jnp.einsum(
        "nk,nc->kc",
        dispatch,
        sample_state.reshape(samples, 2 * state_width),
        preferred_element_type=jnp.float32,
    ).astype(jnp.bfloat16)
    outgoing = outgoing.reshape(groups, local_blocks, slot_bound, 2, state_width)
    block_table = jax.vmap(complex_table)(jnp.transpose(stem_field, (0, 2, 3, 1)))
    result = jnp.einsum(
        "gsmpb,spbqa->gsmqa",
        lax.all_to_all(outgoing, ("ma", "mb"), split_axis=0, concat_axis=0, tiled=True),
        block_table,
        preferred_element_type=jnp.float32,
    ).astype(jnp.bfloat16)
    returned = lax.all_to_all(result, ("ma", "mb"), split_axis=0, concat_axis=0, tiled=True)
    width_out = returned.shape[4]
    gathered_rows = returned.reshape(block_count * slot_bound, 2 * width_out)
    amplitudes = jnp.dot(dispatch, gathered_rows, preferred_element_type=jnp.float32).astype(
        jnp.bfloat16
    )
    return amplitudes.reshape(samples, 2, width_out)


def solution(mesh):
    placed = (
        P(("cuts", "ma", "mb"), None, None, None),
        P(None, None, "ma", None),
        P(None, None, "ma", None),
        P(),
        P(("cuts", "ma", "mb"), None),
        P(("cuts", "ma", "mb"), None, None),
    )
    return jax.shard_map(
        on_device,
        mesh=mesh,
        in_specs=placed,
        out_specs=P(("cuts", "ma", "mb"), None, None),
        check_vma=False,
    )
```

profile of v0, /device:TPU:1, one launch (start us, length us, event | category | flops | bytes accessed | tf_op | source)
XLA Modules:
  0.0 280.3 jit_solution(17453023563885691046)
XLA Ops:
  6.5 0.7 all-gather.3.cloned.1.call-update
  7.3 0.7 all-gather.5.cloned.1.call-update
  8.0 5.4 %copy.33 = bf16[2,16,32,2,512]{4,3,2,0,1:T(2,128)(2,1)} copy(bf16[2,16,32,2,512]{4,3,2,1,0:T(2,128)(2,1)} %bitcast.189) | data formatting | bytes 4194304 | tf_op jit(solution)/shard_map/reshape | solution.py:20
  13.4 7.5 %all-to-all-start = ((bf16[2,16,32,2,512]{4,3,2,0,1:T(2,128)(2,1)}), bf16[2,16,32,2,512]{4,3,2,0,1:T(2,128)(2,1)S(1)}, u32[]{:S(2)}, u32[]{:S(2)}) async-start(bf16[2,16,32,2,512]{4,3,2,0,1:T(2,128)(2,1)} %copy.33), calls=%async_computation | async-start | bytes 4194304 | tf_op jit(solution)/shard_map/all_to_all | solution.py:21
  20.9 64.5 %all-gather.3.cloned.1.call-done = bf16[2,2,512,512]{3,2,1,0:T(8,128)(2,1)} async-done(((bf16[2,2,64,512]{3,2,1,0:T(8,128)(2,1)}), bf16[2,2,512,512]{3,2,1,0:T(8,128)(2,1)}) %all-gather.3.cloned.1.call-update) | async-done | bytes 2097168 | tf_op jit(solution)/shard_map/all_gather | solution.py:31
  85.4 1.9 fusion.20
  87.4 1.1 maximum_bitcast_fusion.11
  88.6 50.2 %all-gather.5.cloned.1.call-done = bf16[2,2,512,512]{3,2,1,0:T(8,128)(2,1)} async-done(((bf16[2,2,64,512]{3,2,1,0:T(8,128)(2,1)}), bf16[2,2,512,512]{3,2,1,0:T(8,128)(2,1)}) %all-gather.5.cloned.1.call-update) | async-done | bytes 2097168 | tf_op jit(solution)/shard_map/all_gather | solution.py:32
  138.8 2.2 fusion.41
  141.0 1.2 slice_bitcast_fusion.8
  142.2 1.5 maximum_bitcast_fusion.13
  143.7 1.8 copy.34
  145.5 7.0 %bitcast_convert_fusion.3 = bf16[2,512,2,512]{3,1,2,0:T(8,128)(2,1)S(1)} fusion(bf16[1,512,2,512]{3,1,0,2:T(8,128)(2,1)} %get-tuple-element.24, bf16[1,512,2,512]{3,1,0,2:T(8,128)(2,1)} %get-tuple-element.23, bf16[2,512,2,512,1]{3,1,4,2,0:T(8,128)(2,1)} %bitcast.190, bf16[1,512,2,512]{3,1,2,0:T(8,128)(2,1)} %get-tuple-element.22, ...), kind=kOutput, calls=%fused_computation.6 | convolution fusion | flops 4305453056 | bytes 8388608 | tf_op jit(solution)/shard_map/sapb,pbqo->saqo/dot_general | solution.py:51
  152.5 1.4 copy.37
  153.9 6.2 %all-to-all-start.1 = ((bf16[2,16,32,2,512]{4,2,3,0,1:T(8,128)(2,1)}), bf16[2,16,32,2,512]{4,2,3,0,1:T(8,128)(2,1)S(1)}, u32[]{:S(2)}, u32[]{:S(2)}) async-start(bf16[2,16,32,2,512]{4,2,3,0,1:T(8,128)(2,1)} %copy.37), calls=%async_computation.1 | async-start | bytes 4194304 | tf_op jit(solution)/shard_map/all_to_all | solution.py:21
  161.0 1.6 reshape.149
  162.6 2.6 copy.42
  165.2 0.7 fusion.19
  165.9 0.8 fusion.39
  166.7 1.0 slice_bitcast_fusion.12
  167.8 34.0 %all-to-all-done.1 = bf16[2,16,32,2,512]{4,2,3,0,1:T(8,128)(2,1)S(1)} async-done(((bf16[2,16,32,2,512]{4,2,3,0,1:T(8,128)(2,1)}), bf16[2,16,32,2,512]{4,2,3,0,1:T(8,128)(2,1)S(1)}, u32[]{:S(2)}, u32[]{:S(2)}) %all-to-all-start.1) | async-done | bytes 2097184 | tf_op jit(solution)/shard_map/all_to_all | solution.py:21
  201.8 10.7 %all-to-all-start.2 = ((bf16[16,2,16,2,512]{4,2,3,1,0:T(8,128)(2,1)}), bf16[16,2,16,2,512]{4,2,3,1,0:T(8,128)(2,1)}, u32[]{:S(2)}, u32[]{:S(2)}) async-start(bf16[16,2,16,2,512]{4,2,3,1,0:T(8,128)(2,1)} %copy.42), calls=%async_computation.2 | async-start | bytes 2097152 | tf_op jit(solution)/shard_map/all_to_all | solution.py:87
  212.4 3.0 %maximum_bitcast_fusion.9 = (bf16[1,512,2,512]{3,1,2,0:T(8,128)(2,1)}, bf16[1,512,2,512]{3,1,2,0:T(8,128)(2,1)}) fusion(bf16[512,1,512]{2,0,1:T(8,128)(2,1)} %get-tuple-element.15, bf16[512,1,512]{2,0,1:T(8,128)(2,1)} %get-tuple-element.16, bf16[512,1,512]{2,0,1:T(8,128)(2,1)S(1)} %copy-done.1), kind=kLoop, calls=%fused_computation.38 | loop fusion | flops 1048576 | bytes 3670016 | tf_op jit(solution)/shard_map/stack | solution.py:12
  215.4 1.6 maximum_bitcast_fusion.15
  217.0 1.5 copy.38
  218.6 7.0 %fusion.12 = bf16[2,2,512,512]{2,3,1,0:T(8,128)(2,1)S(1)} fusion(bf16[2,512,2,512,1]{3,1,4,2,0:T(8,128)(2,1)} %bitcast.191, bf16[1,512,2,512]{3,1,2,0:T(8,128)(2,1)} %get-tuple-element.20, bf16[1,512,2,512]{3,1,2,0:T(8,128)(2,1)S(1)} %copy-done.5, bf16[1,512,2,512]{3,1,2,0:T(8,128)(2,1)} %get-tuple-element.26, bf16[1,512,2,512]{3,1,2,0:T(8,128)(2,1)} %get-tuple-element.25), kind=kOutput, calls=%fused_computation.24 | convolution fusion | flops 4302307328 | bytes 8388608 | tf_op jit(solution)/shard_map/sapb,pbqo->saqo/dot_general | solution.py:51
  225.9 1.7 maximum_bitcast_fusion.7
  227.6 8.1 %all-to-all-done.2 = bf16[16,2,16,2,512]{4,2,3,1,0:T(8,128)(2,1)} async-done(((bf16[16,2,16,2,512]{4,2,3,1,0:T(8,128)(2,1)}), bf16[16,2,16,2,512]{4,2,3,1,0:T(8,128)(2,1)}, u32[]{:S(2)}, u32[]{:S(2)}) %all-to-all-start.2) | async-done | bytes 1048608 | tf_op jit(solution)/shard_map/all_to_all | solution.py:87
  235.7 3.1 %fusion.21 = bf16[16,2,16,2,512]{4,2,0,3,1:T(8,128)(2,1)S(1)} fusion(bf16[1,2,512,2,512]{2,4,1,3,0:T(8,128)(2,1)} %get-tuple-element.14, bf16[1,2,512,2,512]{2,4,1,3,0:T(8,128)(2,1)S(1)} %get-tuple-element.13, bf16[16,2,16,2,512]{4,2,3,1,0:T(8,128)(2,1)} %all-to-all-done.2), kind=kOutput, calls=%fused_computation.30 | convolution fusion | flops 1076363264 | bytes 6291456 | tf_op jit(solution)/shard_map/gsmpb,spbqa->gsmqa/dot_general | solution.py:85
  238.9 31.5 %all_to_all.20 = bf16[16,2,16,2,512]{4,2,3,1,0:T(8,128)(2,1)S(1)} all-to-all(bf16[16,2,16,2,512]{4,2,3,1,0:T(8,128)(2,1)S(1)} %copy.45), channel_id=1, replica_groups=mesh['cuts'=2,'ma'=8,'mb'=2] {'ma','mb'}, dimensions={0} | all-to-all | bytes 2097152 | tf_op jit(solution)/shard_map/all_to_all | solution.py:91
  270.5 1.1 copy.46
  272.3 1.2 reshape.151
  (37 shorter events, 2.0 us)
Async XLA Ops:
  6.5 78.8 %all-gather.3.cloned.1.call-start = ((), (), s32[]{:S(2)}) async-start(), calls=%async_computation.4 | async-start | bytes 2359296 | tf_op jit(solution)/shard_map/all_gather | solution.py:31
  7.3 131.5 %all-gather.5.cloned.1.call-start = ((), (), s32[]{:S(2)}) async-start(), calls=%async_computation.5 | async-start | bytes 2359296 | tf_op jit(solution)/shard_map/all_gather | solution.py:32
  13.4 7.5 %copy-start.7 = (s32[2,512]{1,0:T(2,128)S(1)}, s32[2,512]{1,0:T(2,128)}, u32[]{:S(2)}) copy-start(s32[2,512]{1,0:T(2,128)} %param.9) | copy-start | bytes 12292
  13.4 130.3 %all-to-all-start = ((bf16[2,16,32,2,512]{4,3,2,0,1:T(2,128)(2,1)}), bf16[2,16,32,2,512]{4,3,2,0,1:T(2,128)(2,1)S(1)}, u32[]{:S(2)}, u32[]{:S(2)}) async-start(bf16[2,16,32,2,512]{4,3,2,0,1:T(2,128)(2,1)} %copy.33), calls=%async_computation | async-start | bytes 4194304 | tf_op jit(solution)/shard_map/all_to_all | solution.py:21
  138.8 2.2 copy-start
  153.9 6.2 %copy-start.6 = (bf16[256,2,512]{2,1,0:T(2,128)(2,1)S(1)}, bf16[256,2,512]{2,1,0:T(2,128)(2,1)}, u32[]{:S(2)}) copy-start(bf16[256,2,512]{2,1,0:T(2,128)(2,1)} %param.11) | copy-start | bytes 1572868
  153.9 6.3 %copy-start.8 = (s32[256,1]{0,1:T(1,128)S(1)}, s32[256,1]{0,1:T(1,128)}, u32[]{:S(2)}) copy-start(s32[256,1]{0,1:T(1,128)} %param.10) | copy-start | bytes 3076
  153.9 47.8 %all-to-all-start.1 = ((bf16[2,16,32,2,512]{4,2,3,0,1:T(8,128)(2,1)}), bf16[2,16,32,2,512]{4,2,3,0,1:T(8,128)(2,1)S(1)}, u32[]{:S(2)}, u32[]{:S(2)}) async-start(bf16[2,16,32,2,512]{4,2,3,0,1:T(8,128)(2,1)} %copy.37), calls=%async_computation.1 | async-start | bytes 4194304 | tf_op jit(solution)/shard_map/all_to_all | solution.py:21
  162.6 2.6 copy-start.9
  167.8 44.7 %copy-start.1 = (bf16[512,1,512]{2,0,1:T(8,128)(2,1)S(1)}, bf16[512,1,512]{2,0,1:T(8,128)(2,1)}, u32[]{:S(2)}) copy-start(bf16[512,1,512]{2,0,1:T(8,128)(2,1)} %fusion.39) | copy-start | bytes 1572868
  201.8 33.9 %all-to-all-start.2 = ((bf16[16,2,16,2,512]{4,2,3,1,0:T(8,128)(2,1)}), bf16[16,2,16,2,512]{4,2,3,1,0:T(8,128)(2,1)}, u32[]{:S(2)}, u32[]{:S(2)}) async-start(bf16[16,2,16,2,512]{4,2,3,1,0:T(8,128)(2,1)} %copy.42), calls=%async_computation.2 | async-start | bytes 2097152 | tf_op jit(solution)/shard_map/all_to_all | solution.py:87
  212.4 3.0 %copy-start.2 = (bf16[512,1,512]{2,0,1:T(8,128)(2,1)S(1)}, bf16[512,1,512]{2,0,1:T(8,128)(2,1)}, u32[]{:S(2)}) copy-start(bf16[512,1,512]{2,0,1:T(8,128)(2,1)} %get-tuple-element.12) | copy-start | bytes 1572868
  212.4 3.0 %copy-start.3 = (bf16[512,1,512]{2,0,1:T(8,128)(2,1)S(1)}, bf16[512,1,512]{2,0,1:T(8,128)(2,1)}, u32[]{:S(2)}) copy-start(bf16[512,1,512]{2,0,1:T(8,128)(2,1)} %get-tuple-element.8) | copy-start | bytes 1572868
  212.4 3.0 %copy-start.4 = (bf16[512,1,512]{2,0,1:T(8,128)(2,1)S(1)}, bf16[512,1,512]{2,0,1:T(8,128)(2,1)}, u32[]{:S(2)}) copy-start(bf16[512,1,512]{2,0,1:T(8,128)(2,1)} %get-tuple-element.9) | copy-start | bytes 1572868
  217.0 1.6 copy-start.5
Sparse Core Ops, SparseCore 0:
  9.5 75.8 all-gather.2
  87.6 51.1 all-gather.4
where the time goes:
time: 281 us; the launch traced here: 280 us
  waiting for transfers between devices  158 us (56%)
  blocking collectives  31.5 us (11%)
  starting transfers between devices  24.4 us (9%)
  matrix products  20.9 us (7%)
  local copies, waits for them, and re-layouts  19.5 us (7%)
  between operations  13.6 us (5%)
  other arithmetic  12.2 us (4%)
    all_gather x1, waiting for transfers between devices, on_device(): lax.all_gather(first_branch_tensors, 'ma', axis=2, tiled=True)  64.5 us
    all_gather x1, waiting for transfers between devices, on_device(): lax.all_gather(second_branch_tensors, 'ma', axis=2, tiled=True)  50.2 us
    all_to_all x2, waiting for transfers between devices, regroup(): lax.all_to_all(pieces, ('ma', 'mb'), split_axis=1, concat_axis=1, tiled=T...  34 us
    all_to_all x1, blocking collectives, on_device(): lax.all_to_all(result, ('ma', 'mb'), split_axis=0, concat_axis=0, tiled=T...  31.5 us
    dot_general x2, matrix products, on_device(): jnp.einsum('sapb,pbqo->saqo', stem_field, complex_table(second_matrix), p...  14 us
    all_to_all x2, starting transfers between devices, regroup(): lax.all_to_all(pieces, ('ma', 'mb'), split_axis=1, concat_axis=1, tiled=T...  13.7 us
    all_to_all x1, starting transfers between devices, on_device(): lax.all_to_all(outgoing, ('ma', 'mb'), split_axis=0, concat_axis=0, tiled...  10.7 us
    another operation x5, other arithmetic, complex_table(): return jnp.stack([upper_rows, lower_rows], axis=0)  8.96 us
  transfers between devices with their start and end apart: 5, of which 4 were waited for; matrix products, arithmetic and copies ran while one was open for 13% of the time, Pallas kernels for 0%

commit v1 on v0

--- a/solution.py
+++ b/solution.py
@@ -2,6 +2,22 @@
 import jax.numpy as jnp
 from jax import lax
 from jax.sharding import PartitionSpec as P
+
+
+def swapped_with_each(x, axis, split, join):
+    ways, here = (lax.axis_size(axis), lax.axis_index(axis))
+    width = x.shape[split] // ways
+    shape = list(x.shape)
+    shape[split] = width
+    height = shape[join]
+    shape[join] = height * ways
+    full = jnp.zeros(shape, x.dtype)
+    for mask in range(ways):
+        part = lax.dynamic_slice_in_dim(x, (here ^ mask) * width, width, axis=split)
+        if mask:
+            part = lax.ppermute(part, axis, [(d, d ^ mask) for d in range(ways)])
+        full = lax.dynamic_update_slice_in_dim(full, part, (here ^ mask) * height, axis=join)
+    return full
 
 
 def complex_table(matrix):
@@ -18,7 +34,7 @@
     second_count = lax.axis_size("mb")
     groups = first_count * second_count
     pieces = stem_field.reshape(blocks, groups, row_count // groups, part_count, col_count)
-    swapped_modes = lax.all_to_all(pieces, ("ma", "mb"), split_axis=1, concat_axis=1, tiled=True)
+    swapped_modes = swapped_with_each(pieces, ("ma", "mb"), 1, 1)
     return swapped_modes.reshape(blocks, row_count, part_count, col_count)
 
 

time: 281 us -> 273 us (0.972)
  waiting for transfers between devices: 158 us -> 109 us
  starting transfers between devices: 24.4 us -> 57 us
  blocking collectives: 31.5 us -> 38.9 us
  other arithmetic: 12.2 us -> 8.97 us
    ppermute x0 -> x30, waiting for transfers between devices: none -> 80.9 us  [swapped_with_each(): part = lax.ppermute(part, axis, [(d, d ^ mask) for d in range(ways)])]
    all_gather x1, waiting for transfers between devices: 64.5 us -> 0.02 us  [on_device(): lax.all_gather(first_branch_tensors, 'ma', axis=2, tiled=True)]
    ppermute x0 -> x30, starting transfers between devices: none -> 50.5 us  [swapped_with_each(): part = lax.ppermute(part, axis, [(d, d ^ mask) for d in range(ways)])]
    all_to_all x2 -> x0, waiting for transfers between devices: 34 us -> none  [regroup(): lax.all_to_all(pieces, ('ma', 'mb'), split_axis=1, concat_axis=1, tiled=T...]
    all_gather x1, waiting for transfers between devices: 50.2 us -> 26.6 us  [on_device(): lax.all_gather(second_branch_tensors, 'ma', axis=2, tiled=True)]
    all_to_all x2 -> x0, starting transfers between devices: 13.7 us -> none  [regroup(): lax.all_to_all(pieces, ('ma', 'mb'), split_axis=1, concat_axis=1, tiled=T...]
    all_to_all x1, waiting for transfers between devices: 8.1 us -> 0.01 us  [on_device(): lax.all_to_all(outgoing, ('ma', 'mb'), split_axis=0, concat_axis=0, tiled...]
    all_to_all x1, blocking collectives: 31.5 us -> 38.9 us  [on_device(): lax.all_to_all(result, ('ma', 'mb'), split_axis=0, concat_axis=0, tiled=T...]
  transfers between devices with their start and end apart: 5 -> 33, of which waited for: 4 -> 12; matrix products, arithmetic and copies ran while one was open for 13% -> 16% of each run, Pallas kernels for 0% -> 0%
where the time goes in v1:
time: 273 us; the launch traced here: 272 us
  waiting for transfers between devices  109 us (40%)
  starting transfers between devices  57 us (21%)
  blocking collectives  38.9 us (14%)
  matrix products  22.2 us (8%)
  local copies, waits for them, and re-layouts  22.1 us (8%)
  between operations  14.1 us (5%)
  other arithmetic  8.97 us (3%)
    ppermute x30, waiting for transfers between devices, swapped_with_each(): part = lax.ppermute(part, axis, [(d, d ^ mask) for d in range(ways)])  80.9 us
    ppermute x30, starting transfers between devices, swapped_with_each(): part = lax.ppermute(part, axis, [(d, d ^ mask) for d in range(ways)])  50.5 us
    all_to_all x1, blocking collectives, on_device(): lax.all_to_all(result, ('ma', 'mb'), split_axis=0, concat_axis=0, tiled=T...  38.9 us
    all_gather x1, waiting for transfers between devices, on_device(): lax.all_gather(second_branch_tensors, 'ma', axis=2, tiled=True)  26.6 us
    dot_general x2, matrix products, on_device(): jnp.einsum('sapb,pbqo->saqo', stem_field, complex_table(second_matrix), p...  15.3 us
    another operation x5, other arithmetic, complex_table(): return jnp.stack([upper_rows, lower_rows], axis=0)  7.92 us
    all_to_all x1, starting transfers between devices, on_device(): lax.all_to_all(outgoing, ('ma', 'mb'), split_axis=0, concat_axis=0, tiled...  6.32 us
  transfers between devices with their start and end apart: 33, of which 12 were waited for; matrix products, arithmetic and copies ran while one was open for 16% of the time, Pallas kernels for 0%

profile of v1, /device:TPU:1, one launch (start us, length us, event | category | flops | bytes accessed | tf_op | source)
XLA Modules:
  0.0 272.1 jit_solution(6590454631538353851)
XLA Ops:
  7.4 4.4 %constant_dynamic-slice_fusion.15 = (bf16[2,1,32,2,512]{4,3,2,1,0:T(2,128)(2,1)S(1)}, bf16[2,1,32,2,512]{4,3,2,1,0:T(2,128)(2,1)S(1)}, bf16[2,1,32,2,512]{4,3,2,...) fusion(bf16[2,16,32,2,512]{4,3,2,1,0:T(2,128)(2,1)} %bitcast.19, ...), kind=kLoop, calls=%fused_computation.112 | loop fusion | bytes 4194368 | tf_op jit(solution)/shard_map/dynamic_slice | solution.py:16
  11.8 2.7 collective-permute-start.1
  14.5 1.7 collective-permute-start.3
  19.3 6.3 %all-to-all-start = ((bf16[16,2,16,2,512]{4,2,3,1,0:T(8,128)(2,1)}), bf16[16,2,16,2,512]{4,2,3,1,0:T(8,128)(2,1)}, u32[]{:S(2)}, u32[]{:S(2)}) async-start(bf16[16,2,16,2,512]{4,2,3,1,0:T(8,128)(2,1)} %copy.72), calls=%async_computation | async-start | bytes 2097152 | tf_op jit(solution)/shard_map/all_to_all | solution.py:103
  26.7 2.3 collective-permute-start.5
  31.4 2.6 collective-permute-start.7
  36.2 3.0 %collective-permute-start.9 = (bf16[2,1,32,2,512]{4,3,2,1,0:T(2,128)(2,1)S(1)}, bf16[2,1,32,2,512]{4,3,2,1,0:T(2,128)(2,1)S(1)}, u32[]{:S(2)}, u32[]{:S(2)}) collective-permute-start(bf16[2,1,32,2,512]{4,3,2,1,0:T(2,128)(2,1)S(1)} %get-tuple-element.28), channel_id=1, source_target_pairs={{0,10},{1,11},{2,8},{3,9},{4,14},{5,15},{6,12},{7,13},{8,2},{9,3},... | collective-permute-start | bytes 393224 | tf_op jit(solution)/shard_map/ppermute | solution.py:18
  40.1 14.4 %collective-permute-done.5 = bf16[2,1,32,2,512]{4,3,2,1,0:T(2,128)(2,1)S(1)} collective-permute-done((bf16[2,1,32,2,512]{4,3,2,1,0:T(2,128)(2,1)}, bf16[2,1,32,2,512]{4,3,2,1,0:T(2,128)(2,1)S(1)}, u32[]{:S(2)}, u32[]{:S(2)}) %collective-permute-start.5) | collective-permute-done | bytes 131104 | tf_op jit(solution)/shard_map/ppermute | solution.py:18
  54.6 4.4 %collective-permute-start.10 = (bf16[2,1,32,2,512]{4,3,2,1,0:T(2,128)(2,1)S(1)}, bf16[2,1,32,2,512]{4,3,2,1,0:T(2,128)(2,1)S(1)}, u32[]{:S(2)}, u32[]{:S(2)}) collective-permute-start(bf16[2,1,32,2,512]{4,3,2,1,0:T(2,128)(2,1)S(1)} %get-tuple-element.27), channel_id=1, source_target_pairs={{0,11},{1,10},{2,9},{3,8},{4,15},{5,14},{6,13},{7,12},{8,3},{9,2},... | collective-permute-start | bytes 393224 | tf_op jit(solution)/shard_map/ppermute | solution.py:18
  59.0 4.0 %collective-permute-done.6 = bf16[2,1,32,2,512]{4,3,2,1,0:T(2,128)(2,1)S(1)} collective-permute-done((bf16[2,1,32,2,512]{4,3,2,1,0:T(2,128)(2,1)}, bf16[2,1,32,2,512]{4,3,2,1,0:T(2,128)(2,1)S(1)}, u32[]{:S(2)}, u32[]{:S(2)}) %collective-permute-start.6) | collective-permute-done | bytes 131104 | tf_op jit(solution)/shard_map/ppermute | solution.py:18
  63.0 3.8 %collective-permute-start.11 = (bf16[2,1,32,2,512]{4,3,2,1,0:T(2,128)(2,1)S(1)}, bf16[2,1,32,2,512]{4,3,2,1,0:T(2,128)(2,1)S(1)}, u32[]{:S(2)}, u32[]{:S(2)}) collective-permute-start(bf16[2,1,32,2,512]{4,3,2,1,0:T(2,128)(2,1)S(1)} %get-tuple-element.26), channel_id=1, source_target_pairs={{0,12},{1,13},{2,14},{3,15},{4,8},{5,9},{6,10},{7,11},{8,4},{9,5},... | collective-permute-start | bytes 393224 | tf_op jit(solution)/shard_map/ppermute | solution.py:18
  66.8 22.6 %collective-permute-done.7 = bf16[2,1,32,2,512]{4,3,2,1,0:T(2,128)(2,1)S(1)} collective-permute-done((bf16[2,1,32,2,512]{4,3,2,1,0:T(2,128)(2,1)S(1)}, bf16[2,1,32,2,512]{4,3,2,1,0:T(2,128)(2,1)S(1)}, u32[]{:S(2)}, u32[]{:S(2)}) %collective-permute-start.7) | collective-permute-done | bytes 131104 | tf_op jit(solution)/shard_map/ppermute | solution.py:18
  90.7 2.2 collective-permute-done.8
  92.9 2.0 collective-permute-start.13
  94.9 7.4 %collective-permute-done.9 = bf16[2,1,32,2,512]{4,3,2,1,0:T(2,128)(2,1)S(1)} collective-permute-done((bf16[2,1,32,2,512]{4,3,2,1,0:T(2,128)(2,1)S(1)}, bf16[2,1,32,2,512]{4,3,2,1,0:T(2,128)(2,1)S(1)}, u32[]{:S(2)}, u32[]{:S(2)}) %collective-permute-start.9) | collective-permute-done | bytes 131104 | tf_op jit(solution)/shard_map/ppermute | solution.py:18
  102.2 1.6 collective-permute-start.14
  105.2 8.2 %collective-permute-done.14 = bf16[2,1,32,2,512]{4,3,2,1,0:T(2,128)(2,1)S(1)} collective-permute-done((bf16[2,1,32,2,512]{4,3,2,1,0:T(2,128)(2,1)S(1)}, bf16[2,1,32,2,512]{4,3,2,1,0:T(2,128)(2,1)S(1)}, u32[]{:S(2)}, u32[]{:S(2)}) %collective-permute-start.14) | collective-permute-done | bytes 131104 | tf_op jit(solution)/shard_map/ppermute | solution.py:18
  113.4 1.9 fusion.20
  119.5 26.6 %all-gather.5.cloned.1.call-done = bf16[2,2,512,512]{3,2,1,0:T(8,128)(2,1)} async-done(((bf16[2,2,64,512]{3,2,1,0:T(8,128)(2,1)}), bf16[2,2,512,512]{3,2,1,0:T(8,128)(2,1)}) %all-gather.5.cloned.1.call-update) | async-done | bytes 2097168 | tf_op jit(solution)/shard_map/all_gather | solution.py:48
  146.1 2.8 %slice_bitcast_fusion.8 = (bf16[512,1,512]{2,0,1:T(8,128)(2,1)S(1)}, bf16[512,1,512]{2,0,1:T(8,128)(2,1)}, bf16[512,1,512]{2,0,1:T(8,128)(2,1)}, bf16[512,1,512]{2,0,1:T(8,128)(2,1)S(1)}) fusion(bf16[2,2,512,512]{3,2,1,0:T(8,128)(2,1)} %all-gather.5.cloned.1.call-done), kind=kLoop, calls=%fused_computation.53 | loop fusion | bytes 4194304 | tf_op jit(solution)/shard_map/stack;squeeze | solution.py:26
  151.3 8.1 %bitcast_convert_fusion.3 = bf16[2,512,2,512]{3,1,2,0:T(8,128)(2,1)} fusion(bf16[1,512,2,512]{3,1,0,2:T(8,128)(2,1)} %get-tuple-element.56, bf16[1,512,2,512]{3,1,0,2:T(8,128)(2,1)} %get-tuple-element.55, bf16[2,512,2,512,1]{3,1,4,2,0:T(8,128)(2,1)S(1)} %bitcast.190, bf16[1,512,2,512]{3,1,2,0:T(8,128)(2,1)} %get-tuple-element.54, ...), kind=kOutput, calls=%fused_computation.6 | convolution fusion | flops 4305453056 | bytes 8388608 | tf_op jit(solution)/shard_map/sapb,pbqo->saqo/dot_general | solution.py:67
  176.1 3.4 %collective-permute-start.25 = (bf16[2,1,32,2,512]{4,2,1,3,0:T(8,128)(2,1)S(1)}, bf16[2,1,32,2,512]{4,2,1,3,0:T(8,128)(2,1)S(1)}, u32[]{:S(2)}, u32[]{:S(2)}) collective-permute-start(bf16[2,1,32,2,512]{4,2,1,3,0:T(8,128)(2,1)S(1)} %get-tuple-element.11), channel_id=1, source_target_pairs={{0,11},{1,10},{2,9},{3,8},{4,15},{5,14},{6,13},{7,12},{8,3},{9,2},... | collective-permute-start | bytes 393224 | tf_op jit(solution)/shard_map/ppermute | solution.py:18
  179.5 2.8 %collective-permute-done.21 = bf16[2,1,32,2,512]{4,2,1,3,0:T(8,128)(2,1)S(1)} collective-permute-done((bf16[2,1,32,2,512]{4,2,1,3,0:T(8,128)(2,1)S(1)}, bf16[2,1,32,2,512]{4,2,1,3,0:T(8,128)(2,1)S(1)}, u32[]{:S(2)}, u32[]{:S(2)}) %collective-permute-start.21) | collective-permute-done | bytes 131104 | tf_op jit(solution)/shard_map/ppermute | solution.py:18
  182.3 1.7 collective-permute-start.26
  184.0 1.6 collective-permute-start.27
  185.7 12.8 %collective-permute-done.23 = bf16[2,1,32,2,512]{4,2,1,3,0:T(8,128)(2,1)S(1)} collective-permute-done((bf16[2,1,32,2,512]{4,2,1,3,0:T(8,128)(2,1)S(1)}, bf16[2,1,32,2,512]{4,2,1,3,0:T(8,128)(2,1)S(1)}, u32[]{:S(2)}, u32[]{:S(2)}) %collective-permute-start.23) | collective-permute-done | bytes 131104 | tf_op jit(solution)/shard_map/ppermute | solution.py:18
  200.0 4.1 %collective-permute-start.29 = (bf16[2,1,32,2,512]{4,2,1,3,0:T(8,128)(2,1)S(1)}, bf16[2,1,32,2,512]{4,2,1,3,0:T(8,128)(2,1)S(1)}, u32[]{:S(2)}, u32[]{:S(2)}) collective-permute-start(bf16[2,1,32,2,512]{4,2,1,3,0:T(8,128)(2,1)S(1)} %get-tuple-element.7), channel_id=1, source_target_pairs={{0,15},{1,14},{2,13},{3,12},{4,11},{5,10},{6,9},{7,8},{8,7},{9,6},... | collective-permute-start | bytes 393224 | tf_op jit(solution)/shard_map/ppermute | solution.py:18
  204.2 5.2 %collective-permute-done.25 = bf16[2,1,32,2,512]{4,2,1,3,0:T(8,128)(2,1)S(1)} collective-permute-done((bf16[2,1,32,2,512]{4,2,1,3,0:T(8,128)(2,1)S(1)}, bf16[2,1,32,2,512]{4,2,1,3,0:T(8,128)(2,1)S(1)}, u32[]{:S(2)}, u32[]{:S(2)}) %collective-permute-start.25) | collective-permute-done | bytes 131104 | tf_op jit(solution)/shard_map/ppermute | solution.py:18
  210.9 7.2 %fusion.12 = bf16[2,2,512,512]{2,3,1,0:T(8,128)(2,1)S(1)} fusion(bf16[2,512,2,512,1]{3,1,4,2,0:T(8,128)(2,1)} %bitcast.189, bf16[1,512,2,512]{3,1,2,0:T(8,128)(2,1)} %get-tuple-element.52, bf16[1,512,2,512]{3,1,2,0:T(8,128)(2,1)S(1)} %copy-done.7, bf16[1,512,2,512]{3,1,2,0:T(8,128)(2,1)} %get-tuple-element.58, bf16[1,512,2,512]{3,1,2,0:T(8,128)(2,1)} %get-tuple-element.57), kind=kOutput, calls=%fused_computation.24 | convolution fusion | flops 4302307328 | bytes 8388608 | tf_op jit(solution)/shard_map/sapb,pbqo->saqo/dot_general | solution.py:67
  218.3 1.7 maximum_bitcast_fusion.7
  220.1 3.1 %fusion.21 = bf16[16,2,16,2,512]{4,2,0,3,1:T(8,128)(2,1)S(1)} fusion(bf16[1,2,512,2,512]{2,4,1,3,0:T(8,128)(2,1)} %get-tuple-element.46, bf16[1,2,512,2,512]{2,4,1,3,0:T(8,128)(2,1)S(1)} %get-tuple-element.45, bf16[16,2,16,2,512]{4,2,3,1,0:T(8,128)(2,1)} %all-to-all-done), kind=kOutput, calls=%fused_computation.30 | convolution fusion | flops 1076363264 | bytes 6291456 | tf_op jit(solution)/shard_map/gsmpb,spbqa->gsmqa/dot_general | solution.py:101
  223.3 38.9 %all_to_all.10 = bf16[16,2,16,2,512]{4,2,3,1,0:T(8,128)(2,1)S(1)} all-to-all(bf16[16,2,16,2,512]{4,2,3,1,0:T(8,128)(2,1)S(1)} %copy.75), channel_id=1, replica_groups=mesh['cuts'=2,'ma'=8,'mb'=2] {'ma','mb'}, dimensions={0} | all-to-all | bytes 2097152 | tf_op jit(solution)/shard_map/all_to_all | solution.py:107
  (128 shorter events, 42.4 us)
Async XLA Ops:
  6.5 106.9 %all-gather.3.cloned.1.call-start = ((), (), s32[]{:S(2)}) async-start(), calls=%async_computation.2 | async-start | bytes 2359296 | tf_op jit(solution)/shard_map/all_gather | solution.py:47
  11.7 15.0 %collective-permute-start = (bf16[2,1,32,2,512]{4,3,2,1,0:T(2,128)(2,1)}, bf16[2,1,32,2,512]{4,3,2,1,0:T(2,128)(2,1)}, u32[]{:S(2)}, u32[]{:S(2)}) collective-permute-start(bf16[2,1,32,2,512]{4,3,2,1,0:T(2,128)(2,1)} %get-tuple-element.37), channel_id=1, source_target_pairs={{0,1},{1,0},{2,3},{3,2},{4,5},{5,4},{6,7},{7,6},{8,9},{9,8},{10,11... | collective-permute-start | bytes 393224 | tf_op jit(solution)/shard_map/ppermute | solution.py:18
  11.8 18.2 %collective-permute-start.1 = (bf16[2,1,32,2,512]{4,3,2,1,0:T(2,128)(2,1)}, bf16[2,1,32,2,512]{4,3,2,1,0:T(2,128)(2,1)}, u32[]{:S(2)}, u32[]{:S(2)}) collective-permute-start(bf16[2,1,32,2,512]{4,3,2,1,0:T(2,128)(2,1)} %get-tuple-element.36), channel_id=1, source_target_pairs={{0,2},{1,3},{2,0},{3,1},{4,6},{5,7},{6,4},{7,5},{8,10},{9,11},{10,... | collective-permute-start | bytes 393224 | tf_op jit(solution)/shard_map/ppermute | solution.py:18
  14.5 16.9 %collective-permute-start.2 = (bf16[2,1,32,2,512]{4,3,2,1,0:T(2,128)(2,1)}, bf16[2,1,32,2,512]{4,3,2,1,0:T(2,128)(2,1)}, u32[]{:S(2)}, u32[]{:S(2)}) collective-permute-start(bf16[2,1,32,2,512]{4,3,2,1,0:T(2,128)(2,1)} %get-tuple-element.35), channel_id=1, source_target_pairs={{0,3},{1,2},{2,1},{3,0},{4,7},{5,6},{6,5},{7,4},{8,11},{9,10},{10,... | collective-permute-start | bytes 393224 | tf_op jit(solution)/shard_map/ppermute | solution.py:18
  14.5 20.4 %collective-permute-start.3 = (bf16[2,1,32,2,512]{4,3,2,1,0:T(2,128)(2,1)}, bf16[2,1,32,2,512]{4,3,2,1,0:T(2,128)(2,1)}, u32[]{:S(2)}, u32[]{:S(2)}) collective-permute-start(bf16[2,1,32,2,512]{4,3,2,1,0:T(2,128)(2,1)} %get-tuple-element.34), channel_id=1, source_target_pairs={{0,4},{1,5},{2,6},{3,7},{4,0},{5,1},{6,2},{7,3},{8,12},{9,13},{10,... | collective-permute-start | bytes 393224 | tf_op jit(solution)/shard_map/ppermute | solution.py:18
  16.2 20.0 %collective-permute-start.4 = (bf16[2,1,32,2,512]{4,3,2,1,0:T(2,128)(2,1)}, bf16[2,1,32,2,512]{4,3,2,1,0:T(2,128)(2,1)}, u32[]{:S(2)}, u32[]{:S(2)}) collective-permute-start(bf16[2,1,32,2,512]{4,3,2,1,0:T(2,128)(2,1)} %get-tuple-element.33), channel_id=1, source_target_pairs={{0,5},{1,4},{2,7},{3,6},{4,1},{5,0},{6,3},{7,2},{8,13},{9,12},{10,... | collective-permute-start | bytes 393224 | tf_op jit(solution)/shard_map/ppermute | solution.py:18
  19.3 200.7 %all-to-all-start = ((bf16[16,2,16,2,512]{4,2,3,1,0:T(8,128)(2,1)}), bf16[16,2,16,2,512]{4,2,3,1,0:T(8,128)(2,1)}, u32[]{:S(2)}, u32[]{:S(2)}) async-start(bf16[16,2,16,2,512]{4,2,3,1,0:T(8,128)(2,1)} %copy.72), calls=%async_computation | async-start | bytes 2097152 | tf_op jit(solution)/shard_map/all_to_all | solution.py:103
  25.7 120.4 %all-gather.5.cloned.1.call-start = ((), (), s32[]{:S(2)}) async-start(), calls=%async_computation.3 | async-start | bytes 2359296 | tf_op jit(solution)/shard_map/all_gather | solution.py:48
  26.7 27.8 %collective-permute-start.5 = (bf16[2,1,32,2,512]{4,3,2,1,0:T(2,128)(2,1)}, bf16[2,1,32,2,512]{4,3,2,1,0:T(2,128)(2,1)S(1)}, u32[]{:S(2)}, u32[]{:S(2)}) collective-permute-start(bf16[2,1,32,2,512]{4,3,2,1,0:T(2,128)(2,1)} %get-tuple-element.32), channel_id=1, source_target_pairs={{0,6},{1,7},{2,4},{3,5},{4,2},{5,3},{6,0},{7,1},{8,14},{9,15},{10,... | collective-permute-start | bytes 393224 | tf_op jit(solution)/shard_map/ppermute | solution.py:18
  30.0 33.1 %collective-permute-start.6 = (bf16[2,1,32,2,512]{4,3,2,1,0:T(2,128)(2,1)}, bf16[2,1,32,2,512]{4,3,2,1,0:T(2,128)(2,1)S(1)}, u32[]{:S(2)}, u32[]{:S(2)}) collective-permute-start(bf16[2,1,32,2,512]{4,3,2,1,0:T(2,128)(2,1)} %get-tuple-element.31), channel_id=1, source_target_pairs={{0,7},{1,6},{2,5},{3,4},{4,3},{5,2},{6,1},{7,0},{8,15},{9,14},{10,... | collective-permute-start | bytes 393224 | tf_op jit(solution)/shard_map/ppermute | solution.py:18
  31.4 58.1 %collective-permute-start.7 = (bf16[2,1,32,2,512]{4,3,2,1,0:T(2,128)(2,1)S(1)}, bf16[2,1,32,2,512]{4,3,2,1,0:T(2,128)(2,1)S(1)}, u32[]{:S(2)}, u32[]{:S(2)}) collective-permute-start(bf16[2,1,32,2,512]{4,3,2,1,0:T(2,128)(2,1)S(1)} %get-tuple-element.30), channel_id=1, source_target_pairs={{0,8},{1,9},{2,10},{3,11},{4,12},{5,13},{6,14},{7,15},{8,0},{9,1},... | collective-permute-start | bytes 393224 | tf_op jit(solution)/shard_map/ppermute | solution.py:18
  34.9 58.0 %collective-permute-start.8 = (bf16[2,1,32,2,512]{4,3,2,1,0:T(2,128)(2,1)S(1)}, bf16[2,1,32,2,512]{4,3,2,1,0:T(2,128)(2,1)S(1)}, u32[]{:S(2)}, u32[]{:S(2)}) collective-permute-start(bf16[2,1,32,2,512]{4,3,2,1,0:T(2,128)(2,1)S(1)} %get-tuple-element.29), channel_id=1, source_target_pairs={{0,9},{1,8},{2,11},{3,10},{4,13},{5,12},{6,15},{7,14},{8,1},{9,0},... | collective-permute-start | bytes 393224 | tf_op jit(solution)/shard_map/ppermute | solution.py:18
  36.2 66.0 %collective-permute-start.9 = (bf16[2,1,32,2,512]{4,3,2,1,0:T(2,128)(2,1)S(1)}, bf16[2,1,32,2,512]{4,3,2,1,0:T(2,128)(2,1)S(1)}, u32[]{:S(2)}, u32[]{:S(2)}) collective-permute-start(bf16[2,1,32,2,512]{4,3,2,1,0:T(2,128)(2,1)S(1)} %get-tuple-element.28), channel_id=1, source_target_pairs={{0,10},{1,11},{2,8},{3,9},{4,14},{5,15},{6,12},{7,13},{8,2},{9,3},... | collective-permute-start | bytes 393224 | tf_op jit(solution)/shard_map/ppermute | solution.py:18
  54.6 50.5 %collective-permute-start.10 = (bf16[2,1,32,2,512]{4,3,2,1,0:T(2,128)(2,1)S(1)}, bf16[2,1,32,2,512]{4,3,2,1,0:T(2,128)(2,1)S(1)}, u32[]{:S(2)}, u32[]{:S(2)}) collective-permute-start(bf16[2,1,32,2,512]{4,3,2,1,0:T(2,128)(2,1)S(1)} %get-tuple-element.27), channel_id=1, source_target_pairs={{0,11},{1,10},{2,9},{3,8},{4,15},{5,14},{6,13},{7,12},{8,3},{9,2},... | collective-permute-start | bytes 393224 | tf_op jit(solution)/shard_map/ppermute | solution.py:18
  63.0 42.0 %collective-permute-start.11 = (bf16[2,1,32,2,512]{4,3,2,1,0:T(2,128)(2,1)S(1)}, bf16[2,1,32,2,512]{4,3,2,1,0:T(2,128)(2,1)S(1)}, u32[]{:S(2)}, u32[]{:S(2)}) collective-permute-start(bf16[2,1,32,2,512]{4,3,2,1,0:T(2,128)(2,1)S(1)} %get-tuple-element.26), channel_id=1, source_target_pairs={{0,12},{1,13},{2,14},{3,15},{4,8},{5,9},{6,10},{7,11},{8,4},{9,5},... | collective-permute-start | bytes 393224 | tf_op jit(solution)/shard_map/ppermute | solution.py:18
  89.5 15.6 %collective-permute-start.12 = (bf16[2,1,32,2,512]{4,3,2,1,0:T(2,128)(2,1)S(1)}, bf16[2,1,32,2,512]{4,3,2,1,0:T(2,128)(2,1)S(1)}, u32[]{:S(2)}, u32[]{:S(2)}) collective-permute-start(bf16[2,1,32,2,512]{4,3,2,1,0:T(2,128)(2,1)S(1)} %get-tuple-element.25), channel_id=1, source_target_pairs={{0,13},{1,12},{2,15},{3,14},{4,9},{5,8},{6,11},{7,10},{8,5},{9,4},... | collective-permute-start | bytes 393224 | tf_op jit(solution)/shard_map/ppermute | solution.py:18
  92.9 12.2 %collective-permute-start.13 = (bf16[2,1,32,2,512]{4,3,2,1,0:T(2,128)(2,1)S(1)}, bf16[2,1,32,2,512]{4,3,2,1,0:T(2,128)(2,1)S(1)}, u32[]{:S(2)}, u32[]{:S(2)}) collective-permute-start(bf16[2,1,32,2,512]{4,3,2,1,0:T(2,128)(2,1)S(1)} %get-tuple-element.24), channel_id=1, source_target_pairs={{0,14},{1,15},{2,12},{3,13},{4,10},{5,11},{6,8},{7,9},{8,6},{9,7},... | collective-permute-start | bytes 393224 | tf_op jit(solution)/shard_map/ppermute | solution.py:18
  102.2 11.2 %collective-permute-start.14 = (bf16[2,1,32,2,512]{4,3,2,1,0:T(2,128)(2,1)S(1)}, bf16[2,1,32,2,512]{4,3,2,1,0:T(2,128)(2,1)S(1)}, u32[]{:S(2)}, u32[]{:S(2)}) collective-permute-start(bf16[2,1,32,2,512]{4,3,2,1,0:T(2,128)(2,1)S(1)} %get-tuple-element.23), channel_id=1, source_target_pairs={{0,15},{1,14},{2,13},{3,12},{4,11},{5,10},{6,9},{7,8},{8,7},{9,6},... | collective-permute-start | bytes 393224 | tf_op jit(solution)/shard_map/ppermute | solution.py:18
  161.2 7.7 %collective-permute-start.15 = (bf16[2,1,32,2,512]{4,2,1,3,0:T(8,128)(2,1)S(1)}, bf16[2,1,32,2,512]{4,2,1,3,0:T(8,128)(2,1)S(1)}, u32[]{:S(2)}, u32[]{:S(2)}) collective-permute-start(bf16[2,1,32,2,512]{4,2,1,3,0:T(8,128)(2,1)S(1)} %get-tuple-element.21), channel_id=1, source_target_pairs={{0,1},{1,0},{2,3},{3,2},{4,5},{5,4},{6,7},{7,6},{8,9},{9,8},{10,11... | collective-permute-start | bytes 393224 | tf_op jit(solution)/shard_map/ppermute | solution.py:18
  162.3 7.8 %collective-permute-start.16 = (bf16[2,1,32,2,512]{4,2,1,3,0:T(8,128)(2,1)S(1)}, bf16[2,1,32,2,512]{4,2,1,3,0:T(8,128)(2,1)S(1)}, u32[]{:S(2)}, u32[]{:S(2)}) collective-permute-start(bf16[2,1,32,2,512]{4,2,1,3,0:T(8,128)(2,1)S(1)} %get-tuple-element.20), channel_id=1, source_target_pairs={{0,2},{1,3},{2,0},{3,1},{4,6},{5,7},{6,4},{7,5},{8,10},{9,11},{10,... | collective-permute-start | bytes 393224 | tf_op jit(solution)/shard_map/ppermute | solution.py:18
  162.6 9.1 %collective-permute-start.17 = (bf16[2,1,32,2,512]{4,2,1,3,0:T(8,128)(2,1)S(1)}, bf16[2,1,32,2,512]{4,2,1,3,0:T(8,128)(2,1)S(1)}, u32[]{:S(2)}, u32[]{:S(2)}) collective-permute-start(bf16[2,1,32,2,512]{4,2,1,3,0:T(8,128)(2,1)S(1)} %get-tuple-element.19), channel_id=1, source_target_pairs={{0,3},{1,2},{2,1},{3,0},{4,7},{5,6},{6,5},{7,4},{8,11},{9,10},{10,... | collective-permute-start | bytes 393224 | tf_op jit(solution)/shard_map/ppermute | solution.py:18
  164.0 9.2 %collective-permute-start.18 = (bf16[2,1,32,2,512]{4,2,1,3,0:T(8,128)(2,1)S(1)}, bf16[2,1,32,2,512]{4,2,1,3,0:T(8,128)(2,1)S(1)}, u32[]{:S(2)}, u32[]{:S(2)}) collective-permute-start(bf16[2,1,32,2,512]{4,2,1,3,0:T(8,128)(2,1)S(1)} %get-tuple-element.18), channel_id=1, source_target_pairs={{0,4},{1,5},{2,6},{3,7},{4,0},{5,1},{6,2},{7,3},{8,12},{9,13},{10,... | collective-permute-start | bytes 393224 | tf_op jit(solution)/shard_map/ppermute | solution.py:18
  165.2 9.3 %collective-permute-start.19 = (bf16[2,1,32,2,512]{4,2,1,3,0:T(8,128)(2,1)S(1)}, bf16[2,1,32,2,512]{4,2,1,3,0:T(8,128)(2,1)S(1)}, u32[]{:S(2)}, u32[]{:S(2)}) collective-permute-start(bf16[2,1,32,2,512]{4,2,1,3,0:T(8,128)(2,1)S(1)} %get-tuple-element.17), channel_id=1, source_target_pairs={{0,5},{1,4},{2,7},{3,6},{4,1},{5,0},{6,3},{7,2},{8,13},{9,12},{10,... | collective-permute-start | bytes 393224 | tf_op jit(solution)/shard_map/ppermute | solution.py:18
  170.1 12.2 %collective-permute-start.21 = (bf16[2,1,32,2,512]{4,2,1,3,0:T(8,128)(2,1)S(1)}, bf16[2,1,32,2,512]{4,2,1,3,0:T(8,128)(2,1)S(1)}, u32[]{:S(2)}, u32[]{:S(2)}) collective-permute-start(bf16[2,1,32,2,512]{4,2,1,3,0:T(8,128)(2,1)S(1)} %get-tuple-element.15), channel_id=1, source_target_pairs={{0,7},{1,6},{2,5},{3,4},{4,3},{5,2},{6,1},{7,0},{8,15},{9,14},{10,... | collective-permute-start | bytes 393224 | tf_op jit(solution)/shard_map/ppermute | solution.py:18
  171.7 12.4 %collective-permute-start.22 = (bf16[2,1,32,2,512]{4,2,1,3,0:T(8,128)(2,1)S(1)}, bf16[2,1,32,2,512]{4,2,1,3,0:T(8,128)(2,1)S(1)}, u32[]{:S(2)}, u32[]{:S(2)}) collective-permute-start(bf16[2,1,32,2,512]{4,2,1,3,0:T(8,128)(2,1)S(1)} %get-tuple-element.14), channel_id=1, source_target_pairs={{0,8},{1,9},{2,10},{3,11},{4,12},{5,13},{6,14},{7,15},{8,0},{9,1},... | collective-permute-start | bytes 393224 | tf_op jit(solution)/shard_map/ppermute | solution.py:18
  173.3 25.2 %collective-permute-start.23 = (bf16[2,1,32,2,512]{4,2,1,3,0:T(8,128)(2,1)S(1)}, bf16[2,1,32,2,512]{4,2,1,3,0:T(8,128)(2,1)S(1)}, u32[]{:S(2)}, u32[]{:S(2)}) collective-permute-start(bf16[2,1,32,2,512]{4,2,1,3,0:T(8,128)(2,1)S(1)} %get-tuple-element.13), channel_id=1, source_target_pairs={{0,9},{1,8},{2,11},{3,10},{4,13},{5,12},{6,15},{7,14},{8,1},{9,0},... | collective-permute-start | bytes 393224 | tf_op jit(solution)/shard_map/ppermute | solution.py:18
  174.5 25.5 %collective-permute-start.24 = (bf16[2,1,32,2,512]{4,2,1,3,0:T(8,128)(2,1)S(1)}, bf16[2,1,32,2,512]{4,2,1,3,0:T(8,128)(2,1)S(1)}, u32[]{:S(2)}, u32[]{:S(2)}) collective-permute-start(bf16[2,1,32,2,512]{4,2,1,3,0:T(8,128)(2,1)S(1)} %get-tuple-element.12), channel_id=1, source_target_pairs={{0,10},{1,11},{2,8},{3,9},{4,14},{5,15},{6,12},{7,13},{8,2},{9,3},... | collective-permute-start | bytes 393224 | tf_op jit(solution)/shard_map/ppermute | solution.py:18
  176.1 33.3 %collective-permute-start.25 = (bf16[2,1,32,2,512]{4,2,1,3,0:T(8,128)(2,1)S(1)}, bf16[2,1,32,2,512]{4,2,1,3,0:T(8,128)(2,1)S(1)}, u32[]{:S(2)}, u32[]{:S(2)}) collective-permute-start(bf16[2,1,32,2,512]{4,2,1,3,0:T(8,128)(2,1)S(1)} %get-tuple-element.11), channel_id=1, source_target_pairs={{0,11},{1,10},{2,9},{3,8},{4,15},{5,14},{6,13},{7,12},{8,3},{9,2},... | collective-permute-start | bytes 393224 | tf_op jit(solution)/shard_map/ppermute | solution.py:18
  182.3 27.1 %collective-permute-start.26 = (bf16[2,1,32,2,512]{4,2,1,3,0:T(8,128)(2,1)S(1)}, bf16[2,1,32,2,512]{4,2,1,3,0:T(8,128)(2,1)S(1)}, u32[]{:S(2)}, u32[]{:S(2)}) collective-permute-start(bf16[2,1,32,2,512]{4,2,1,3,0:T(8,128)(2,1)S(1)} %get-tuple-element.10), channel_id=1, source_target_pairs={{0,12},{1,13},{2,14},{3,15},{4,8},{5,9},{6,10},{7,11},{8,4},{9,5},... | collective-permute-start | bytes 393224 | tf_op jit(solution)/shard_map/ppermute | solution.py:18
  184.0 25.4 %collective-permute-start.27 = (bf16[2,1,32,2,512]{4,2,1,3,0:T(8,128)(2,1)S(1)}, bf16[2,1,32,2,512]{4,2,1,3,0:T(8,128)(2,1)S(1)}, u32[]{:S(2)}, u32[]{:S(2)}) collective-permute-start(bf16[2,1,32,2,512]{4,2,1,3,0:T(8,128)(2,1)S(1)} %get-tuple-element.9), channel_id=1, source_target_pairs={{0,13},{1,12},{2,15},{3,14},{4,9},{5,8},{6,11},{7,10},{8,5},{9,4},... | collective-permute-start | bytes 393224 | tf_op jit(solution)/shard_map/ppermute | solution.py:18
  198.4 11.0 %collective-permute-start.28 = (bf16[2,1,32,2,512]{4,2,1,3,0:T(8,128)(2,1)S(1)}, bf16[2,1,32,2,512]{4,2,1,3,0:T(8,128)(2,1)S(1)}, u32[]{:S(2)}, u32[]{:S(2)}) collective-permute-start(bf16[2,1,32,2,512]{4,2,1,3,0:T(8,128)(2,1)S(1)} %get-tuple-element.8), channel_id=1, source_target_pairs={{0,14},{1,15},{2,12},{3,13},{4,10},{5,11},{6,8},{7,9},{8,6},{9,7},... | collective-permute-start | bytes 393224 | tf_op jit(solution)/shard_map/ppermute | solution.py:18
  200.0 9.5 %collective-permute-start.29 = (bf16[2,1,32,2,512]{4,2,1,3,0:T(8,128)(2,1)S(1)}, bf16[2,1,32,2,512]{4,2,1,3,0:T(8,128)(2,1)S(1)}, u32[]{:S(2)}, u32[]{:S(2)}) collective-permute-start(bf16[2,1,32,2,512]{4,2,1,3,0:T(8,128)(2,1)S(1)} %get-tuple-element.7), channel_id=1, source_target_pairs={{0,15},{1,14},{2,13},{3,12},{4,11},{5,10},{6,9},{7,8},{8,7},{9,6},... | collective-permute-start | bytes 393224 | tf_op jit(solution)/shard_map/ppermute | solution.py:18
  (13 other events, 106.4 us)
Sparse Core Ops, SparseCore 0:
  9.5 81.2 all-gather.2
  93.0 52.9 all-gather.4
